TPU v7x, 32 devices: a whole 2x2x4 slice. The times are simulated.
32 devices in a mesh: prefix: 4 (over z), resp: 8 (over y, x, core).
Axes of the slice: x: 2, y: 2, z: 4, core: 2. Of those that a mesh axis runs over, the one named last changes fastest.
Arguments:
- prompt_kv: bfloat16 [2, 128, 512], P(None, 'prefix'), may hold values from -6 to 6
- response_queries: bfloat16 [64, 128, 1792], P(('prefix', 'resp')), may hold values from -300 to 300
- resp_kv: bfloat16 [64, 128, 512], P(('prefix', 'resp')), may hold values from -6 to 6
- readout: bfloat16 [64, 128, 1792], P(('prefix', 'resp')), may hold values from -3 to 3
- slot_response: int32 [64], P(('prefix', 'resp')), may hold values from 0 to 63, each once
- lengths: int32 [64], replicated, may hold values from 32 to 128
- pair_prompt: int32 [32], replicated, may hold values from 0 to 1
- ref_margin: float32 [32], replicated, may hold values from -60 to 60
Outputs:
- margins: float32 [32], replicated
- grad_q: bfloat16 [64, 128, 1792], P(('prefix', 'resp'))
- grad_resp_kv: bfloat16 [64, 128, 512], P(('prefix', 'resp'))
- grad_prompt_kv: bfloat16 [2, 128, 512], P(None, 'prefix')
Inputs may be any that keep to these rules, and one draw needn't show every extreme that they name: `slot_response`: each response appears in exactly one slot; response 2 k is the chosen and 2 k + 1 the rejected response of pair k.
All inputs are finite; a program needn't handle non-finite values.
Results may differ from a plain program's by a relative error of at most 0.015.
Values may be sent and summed in bfloat16 or wider, within the bound.
A program may use at most 64 MiB of HBM per device.

v0:
```python
import jax
import jax.numpy as jnp
from jax import lax
from jax.sharding import PartitionSpec as P

QUERY_HEADS = 14
KEY_VALUE_HEADS = 2
HEAD_SIZE = 128
margin_beta = 0.1
loss_scale = 256.0


def unpack(packed_rows):
    row_block = packed_rows.shape[0]
    head_width = packed_rows.shape[1] // 2
    key_rows = packed_rows[:, :head_width].reshape(row_block, KEY_VALUE_HEADS, HEAD_SIZE)
    value_rows = packed_rows[:, head_width:].reshape(row_block, KEY_VALUE_HEADS, HEAD_SIZE)
    return (key_rows, value_rows)


def forward_pieces(query_rows, prompt_packed, own_packed, causal):
    prompt_keys, prompt_values = unpack(prompt_packed)
    own_keys, own_values = unpack(own_packed)
    scale_factor = HEAD_SIZE ** (-0.5)
    prompt_scores = (
        jnp.einsum("tgjd,kgd->gjtk", query_rows, prompt_keys, preferred_element_type=jnp.float32)
        * scale_factor
    )
    own_scores = (
        jnp.einsum("tgjd,kgd->gjtk", query_rows, own_keys, preferred_element_type=jnp.float32)
        * scale_factor
    )
    own_scores = jnp.where(causal, own_scores, -jnp.inf)
    row_max = jnp.maximum(
        jnp.max(prompt_scores, -1, keepdims=True), jnp.max(own_scores, -1, keepdims=True)
    )
    prompt_exp = jnp.exp(prompt_scores - row_max)
    own_exp = jnp.exp(own_scores - row_max)
    total = jnp.sum(prompt_exp, -1, keepdims=True) + jnp.sum(own_exp, -1, keepdims=True)
    prefix_probabilities = (prompt_exp / total).astype(jnp.bfloat16)
    self_probabilities = (own_exp / total).astype(jnp.bfloat16)
    attended = jnp.einsum(
        "gjtk,kgd->tgjd", prefix_probabilities, prompt_values, preferred_element_type=jnp.float32
    )
    attended = attended + jnp.einsum(
        "gjtk,kgd->tgjd", self_probabilities, own_values, preferred_element_type=jnp.float32
    )
    return (
        prompt_keys,
        prompt_values,
        own_keys,
        own_values,
        prefix_probabilities,
        self_probabilities,
        attended,
    )


def on_device(
    prompt_kv, response_queries, resp_kv, readout, slot_response, lengths, pair_prompt, ref_margin
):
    prompts = prompt_kv.shape[0]
    slots, slot_capacity, query_width = response_queries.shape
    query_groups = QUERY_HEADS // KEY_VALUE_HEADS
    pairs = ref_margin.shape[0]
    scale_factor = HEAD_SIZE ** (-0.5)
    full_kv = lax.all_gather(prompt_kv, "prefix", axis=1, tiled=True)
    prefix_length = full_kv.shape[1]
    positions = jnp.arange(slot_capacity)
    causal = positions[None, :] <= positions[:, None]
    pair_ids = jnp.arange(pairs)
    prompt_ids = jnp.arange(prompts)
    contrib = jnp.zeros((pairs,), jnp.float32)
    saved = []
    for position_index in range(slots):
        response = slot_response[position_index]
        pair_index = response // 2
        sign = 1.0 - 2.0 * (response % 2).astype(jnp.float32)
        valid = (positions < lengths[response]).astype(jnp.float32)
        prompt_index = pair_prompt[pair_index]
        prompt_packed = lax.dynamic_index_in_dim(full_kv, prompt_index, 0, keepdims=False)
        query_rows = response_queries[position_index].reshape(
            slot_capacity, KEY_VALUE_HEADS, query_groups, HEAD_SIZE
        )
        output_rows = readout[position_index].reshape(
            slot_capacity, KEY_VALUE_HEADS, query_groups, HEAD_SIZE
        )
        pieces = forward_pieces(query_rows, prompt_packed, resp_kv[position_index], causal)
        token_logp = jnp.sum(pieces[-1] * output_rows.astype(jnp.float32), axis=(1, 2, 3)) * valid
        contrib = contrib + jnp.where(pair_ids == pair_index, sign * jnp.sum(token_logp), 0.0)
        saved.append((pair_index, sign, valid, prompt_index, query_rows, output_rows, pieces))
    pair_sums = lax.psum(contrib, ("prefix", "resp"))
    margins = margin_beta * (pair_sums - ref_margin)
    weights = -loss_scale * margin_beta * jax.nn.sigmoid(-margins)
    partial_value = jnp.zeros((prompts, prefix_length, full_kv.shape[2]), jnp.float32)
    grad_rows = []
    grad_own = []
    for pair_index, sign, valid, prompt_index, query_rows, output_rows, pieces in saved:
        (
            prompt_keys,
            prompt_values,
            own_keys,
            own_values,
            prefix_probabilities,
            self_probabilities,
            attended,
        ) = pieces
        coefficient = weights[pair_index] * sign
        output_gradient = (
            coefficient * output_rows.astype(jnp.float32) * valid[:, None, None, None]
        ).astype(jnp.bfloat16)
        prompt_dprobs = jnp.einsum(
            "tgjd,kgd->gjtk", output_gradient, prompt_values, preferred_element_type=jnp.float32
        )
        own_dprobs = jnp.einsum(
            "tgjd,kgd->gjtk", output_gradient, own_values, preferred_element_type=jnp.float32
        )
        delta = jnp.transpose(
            jnp.sum(output_gradient.astype(jnp.float32) * attended, -1), (1, 2, 0)
        )[..., None]
        prefix_score_gradient = (
            prefix_probabilities.astype(jnp.float32) * (prompt_dprobs - delta) * scale_factor
        ).astype(jnp.bfloat16)
        self_score_gradient = (
            self_probabilities.astype(jnp.float32) * (own_dprobs - delta) * scale_factor
        ).astype(jnp.bfloat16)
        grad_queries = jnp.einsum(
            "gjtk,kgd->tgjd", prefix_score_gradient, prompt_keys, preferred_element_type=jnp.float32
        )
        grad_queries = grad_queries + jnp.einsum(
            "gjtk,kgd->tgjd", self_score_gradient, own_keys, preferred_element_type=jnp.float32
        )
        prompt_grad = jnp.concatenate(
            [
                jnp.einsum(
                    "hybi,bhyu->ihu",
                    prefix_score_gradient,
                    query_rows,
                    preferred_element_type=jnp.float32,
                ).reshape(prefix_length, KEY_VALUE_HEADS * HEAD_SIZE),
                jnp.einsum(
                    "hybi,bhyu->ihu",
                    prefix_probabilities,
                    output_gradient,
                    preferred_element_type=jnp.float32,
                ).reshape(prefix_length, KEY_VALUE_HEADS * HEAD_SIZE),
            ],
            axis=-1,
        )
        own_grad = jnp.concatenate(
            [
                jnp.einsum(
                    "hybi,bhyu->ihu",
                    self_score_gradient,
                    query_rows,
                    preferred_element_type=jnp.float32,
                ).reshape(slot_capacity, KEY_VALUE_HEADS * HEAD_SIZE),
                jnp.einsum(
                    "hybi,bhyu->ihu",
                    self_probabilities,
                    output_gradient,
                    preferred_element_type=jnp.float32,
                ).reshape(slot_capacity, KEY_VALUE_HEADS * HEAD_SIZE),
            ],
            axis=-1,
        )
        selector = (prompt_ids == prompt_index)[:, None, None]
        partial_value = partial_value + jnp.where(selector, prompt_grad[None], 0.0)
        grad_rows.append(grad_queries.reshape(slot_capacity, query_width).astype(jnp.bfloat16))
        grad_own.append(own_grad.astype(jnp.bfloat16))
    owned = lax.psum_scatter(partial_value, "prefix", scatter_dimension=1, tiled=True)
    grad_prompt = lax.psum(owned, "resp").astype(jnp.bfloat16)
    return (margins, jnp.stack(grad_rows), jnp.stack(grad_own), grad_prompt)


def solution(mesh):
    in_specs = (
        P(None, "prefix", None),
        P(("prefix", "resp"), None, None),
        P(("prefix", "resp"), None, None),
        P(("prefix", "resp"), None, None),
        P(("prefix", "resp")),
        P(),
        P(),
        P(),
    )
    out_specs = (
        P(),
        P(("prefix", "resp"), None, None),
        P(("prefix", "resp"), None, None),
        P(None, "prefix", None),
    )
    return jax.shard_map(
        on_device, mesh=mesh, in_specs=in_specs, out_specs=out_specs, check_vma=False
    )
```

profile of v0, /device:TPU:0, one launch (start us, length us, event | category | flops | bytes accessed | tf_op | source)
XLA Modules:
  0.0 167.4 jit_solution(1739317058117866416)
XLA Ops:
  7.2 1.3 fusion.48
  15.1 0.6 fusion.47
  18.3 1.9 %iota_compare_fusion.1 = (pred[2]{0:T(512)(128)(4,1)}, pred[2]{0:T(512)(128)(4,1)}) fusion(s32[]{:T(128)} %bitcast.23, s32[]{:T(128)} %bitcast.2), kind=kLoop, calls=%fused_computation.89 | loop fusion | flops 4 | bytes 12 | tf_op jit(solution)/shard_map/eq | solution.py:167
  21.5 0.6 copy-done.24
  22.2 0.6 fusion.46
  22.8 1.2 compare_convert_fusion.1
  24.0 15.6 %all_gather.3 = bf16[2,128,512]{2,1,0:T(8,128)(2,1)S(1)} all-gather(bf16[2,32,512]{2,1,0:T(8,128)(2,1)S(1)} %copy-done.20), channel_id=1, replica_groups=mesh['prefix'=4,'resp'=8] {'prefix'}, dimensions={1}, use_global_device_ids=true | all-gather | bytes 327680 | tf_op jit(solution)/shard_map/all_gather | solution.py:67
  41.5 0.4 copy-done.18
  42.2 0.6 fusion.44
  44.1 0.3 fusion.35
  44.5 1.1 divide_convert_fusion.1
  46.3 0.3 fusion.33
  47.0 0.8 copy-done.12
  47.8 1.5 slice_convert_fusion.1
  49.3 1.5 copy.68
  51.1 1.2 multiply_reduce_fusion.3
  52.3 1.2 fusion.36
  53.5 1.5 copy.79
  55.0 2.0 %convolution_bitcast_fusion.2 = f32[128,2,7,128]{0,3,2,1:T(8,128)} fusion(bf16[128,2,128,1]{0,2,3,1:T(8,128)(2,1)} %bitcast.294, bf16[2,7,128,128]{2,3,1,0:T(8,128)(2,1)S(1)} %get-tuple-element.33), kind=kOutput, calls=%fused_computation.2 | convolution fusion | flops 58720256 | bytes 1441792 | tf_op jit(solution)/shard_map/gjtk,kgd->tgjd/dot_general | solution.py:45
  57.6 2.6 %multiply_reduce_fusion.2 = (f32[128]{0:T(128)S(1)}, f32[128,2,7,128]{0,3,2,1:T(8,128)}) fusion(f32[128,2,7,128]{0,3,2,1:T(8,128)S(1)} %bitcast.278, f32[128,2,7,128]{0,3,2,1:T(8,128)} %convolution_bitcast_fusion.2, bf16[128,2,128,1]{0,2,3,1:T(8,128)(2,1)S(1)} %bitcast.284, bf16[2,7,128,128]{2,3,1,0:T(8,128)(2,1)} %get-tuple-element.32), kind=kOutput, calls=%fused_computation.57 | convolution fusion | flops 59408256 | bytes 3277312 | tf_op jit(solution)/shard_map/gjtk,kgd->tgjd/dot_general | solution.py:42
  60.2 1.2 fusion.37
  62.1 0.6 compare_convert_fusion
  62.7 40.7 %psum.14 = f32[32]{0:T(128)S(1)} all-reduce(f32[32]{0:T(128)S(1)} %fusion.38), channel_id=1, replica_groups=mesh['prefix'=4,'resp'=8] {'prefix','resp'}, use_global_device_ids=true, to_apply=%region_12.13 | all-reduce | flops 32 | bytes 256 | tf_op jit(solution)/shard_map/psum | solution.py:92
  103.4 0.5 divide_multiply_fusion
  103.9 0.6 fusion.45
  105.6 0.6 copy-done.26
  106.2 1.4 multiply_reduce_fusion.1
  108.0 0.4 fusion.25
  108.6 0.5 copy-done.7
  109.3 1.4 multiply_reduce_fusion
  111.0 0.4 fusion.23
  111.7 0.5 copy-done.9
  112.3 0.6 copy-done.21
  113.0 0.9 select_add_fusion
  114.0 1.0 copy-done.3
  115.0 0.9 fusion.29
  115.9 0.4 fusion.24
  116.3 0.6 copy-done.1
  117.2 0.5 copy-done.13
  117.7 0.4 fusion.22
  118.7 0.6 copy-done.19
  120.1 0.4 copy-done.10
  120.4 0.4 copy-done.17
  121.6 0.7 copy-done.8
  122.8 0.7 maximum_maximum_fusion
  123.5 1.0 pad_maximum_fusion
  124.6 11.3 %reduce-scatter.2.cloned.1.call-done = f32[2,32,512]{2,1,0:T(8,128)} async-done(((f32[2,128,512]{2,1,0:T(8,128)}), f32[2,32,512]{2,1,0:T(8,128)}) %reduce-scatter.2.cloned.1.call-update) | async-done | bytes 131088 | tf_op jit(solution)/shard_map/reduce_scatter | solution.py:171
  135.9 24.7 %all-reduce.1 = bf16[2,32,512]{2,1,0:T(8,128)(2,1)} all-reduce(f32[2,32,512]{2,1,0:T(8,128)} %reduce-scatter.2.cloned.1.call-done), channel_id=1, replica_groups=mesh['prefix'=4,'resp'=8] {'resp'}, use_global_device_ids=true, to_apply=%region_16.17 | all-reduce | flops 32768 | bytes 196608 | tf_op jit(solution)/shard_map/psum | solution.py:172
  (88 shorter events, 7.9 us)
Async XLA Ops:
  7.2 128.7 %reduce-scatter.2.cloned.1.call-start = ((), (), s32[]{:S(2)}) async-start(), calls=%async_computation.1 | async-start | bytes 655360 | tf_op jit(solution)/shard_map/reduce_scatter | solution.py:171
  11.8 3.3 %copy-start.23 = (s32[32]{0:T(128)S(1)}, s32[32]{0:T(128)}, u32[]{:S(2)}) copy-start(s32[32]{0:T(128)} %param.14) | copy-start | bytes 388
  11.8 12.2 %copy-start.20 = (bf16[2,32,512]{2,1,0:T(8,128)(2,1)S(1)}, bf16[2,32,512]{2,1,0:T(8,128)(2,1)}, u32[]{:S(2)}) copy-start(bf16[2,32,512]{2,1,0:T(8,128)(2,1)} %param.8) | copy-start | bytes 196612
  21.5 0.7 copy-start.24
  41.0 1.0 copy-start.18
  41.2 4.7 %copy-start.14 = (bf16[128,256]{0,1:T(8,128)(2,1)}, bf16[128,256]{0,1:T(8,128)(2,1)S(1)}, u32[]{:S(2)}) copy-start(bf16[128,256]{0,1:T(8,128)(2,1)S(1)} %copy.59) | copy-start | bytes 196612
  41.2 1.6 copy-start.11
  41.4 2.1 %copy-start.16 = (bf16[128,256]{0,1:T(8,128)(2,1)}, bf16[128,256]{0,1:T(8,128)(2,1)S(1)}, u32[]{:S(2)}) copy-start(bf16[128,256]{0,1:T(8,128)(2,1)S(1)} %copy.70) | copy-start | bytes 196612
  45.6 9.4 %copy-start = (bf16[2,7,128,128]{2,3,1,0:T(8,128)(2,1)}, bf16[2,7,128,128]{2,3,1,0:T(8,128)(2,1)S(1)}, u32[]{:S(2)}) copy-start(bf16[2,7,128,128]{2,3,1,0:T(8,128)(2,1)S(1)} %get-tuple-element.33) | copy-start | bytes 1376260
  46.7 1.2 copy-start.12
  47.8 3.0 %copy-start.2 = (bf16[2,7,128,128]{2,3,1,0:T(8,128)(2,1)}, bf16[2,7,128,128]{2,3,1,0:T(8,128)(2,1)S(1)}, u32[]{:S(2)}) copy-start(bf16[2,7,128,128]{2,3,1,0:T(8,128)(2,1)S(1)} %get-tuple-element.31) | copy-start | bytes 1376260
  47.8 3.2 %copy-start.5 = (bf16[2,7,128,128]{2,3,1,0:T(8,128)(2,1)}, bf16[2,7,128,128]{2,3,1,0:T(8,128)(2,1)S(1)}, u32[]{:S(2)}) copy-start(bf16[2,7,128,128]{2,3,1,0:T(8,128)(2,1)S(1)} %get-tuple-element.30) | copy-start | bytes 1376260
  62.7 40.7 %copy-start.25 = (f32[32]{0:T(128)S(1)}, f32[32]{0:T(128)}, u32[]{:S(2)}) copy-start(f32[32]{0:T(128)} %param.15) | copy-start | bytes 388
  105.6 0.6 copy-start.26
  106.2 1.4 copy-start.6
  108.3 0.8 copy-start.7
  109.3 1.4 copy-start.4
  111.4 0.8 copy-start.9
  112.3 0.6 copy-start.21
  112.3 0.7 copy-start.22
  113.9 1.0 copy-start.3
  115.9 1.0 copy-start.1
  116.9 0.8 copy-start.13
  118.4 0.8 copy-start.19
  119.4 1.0 copy-start.10
  119.9 0.9 copy-start.17
  121.3 1.0 copy-start.8
  121.3 1.0 copy-start.15
Sparse Core Ops, SparseCore 0:
  114.1 21.7 reduce-scatter.1
where the time goes:
time: 169 us; the launch traced here: 167 us
  blocking collectives  81 us (48%)
  between operations  28.7 us (17%)
  local copies, waits for them, and re-layouts  17.5 us (10%)
  other arithmetic  15.8 us (9%)
  matrix products  13 us (8%)
  waiting for transfers between devices  11.4 us (7%)
    psum x1, blocking collectives, on_device(): pair_sums = lax.psum(contrib, ('prefix', 'resp'))  40.7 us
    psum x1, blocking collectives, on_device(): grad_prompt = lax.psum(owned, 'resp').astype(jnp.bfloat16)  24.7 us
    all_gather x1, blocking collectives, on_device(): full_kv = lax.all_gather(prompt_kv, 'prefix', axis=1, tiled=True)  15.6 us
    reduce_scatter x1, waiting for transfers between devices, on_device(): lax.psum_scatter(partial_value, 'prefix', scatter_dimension=1, tiled=True)  11.3 us
    unnamed x58, local copies, waits for them, and re-layouts  9.16 us
    dot_general x2, matrix products, forward_pieces(): jnp.einsum('gjtk,kgd->tgjd', prefix_probabilities, prompt_values, preferr...  3.82 us
  transfers between devices with their start and end apart: 1, of which 1 were waited for; matrix products, arithmetic and copies ran while one was open for 4% of the time, Pallas kernels for 0%

commit v1 on v0

--- a/solution.py
+++ b/solution.py
@@ -89,7 +89,7 @@
         token_logp = jnp.sum(pieces[-1] * output_rows.astype(jnp.float32), axis=(1, 2, 3)) * valid
         contrib = contrib + jnp.where(pair_ids == pair_index, sign * jnp.sum(token_logp), 0.0)
         saved.append((pair_index, sign, valid, prompt_index, query_rows, output_rows, pieces))
-    pair_sums = lax.psum(contrib, ("prefix", "resp"))
+    pair_sums = lax.psum(lax.psum(contrib, "resp"), "prefix")
     margins = margin_beta * (pair_sums - ref_margin)
     weights = -loss_scale * margin_beta * jax.nn.sigmoid(-margins)
     partial_value = jnp.zeros((prompts, prefix_length, full_kv.shape[2]), jnp.float32)

time: 169 us -> 148 us (0.88)
  blocking collectives: 81 us -> 64.4 us
  waiting for transfers between devices: 11.4 us -> 8.75 us
  matrix products: 13 us -> 10.8 us
    psum x1 -> x2, blocking collectives: 40.7 us -> 24.1 us  [on_device(): pair_sums = lax.psum(lax.psum(contrib, 'resp'), 'prefix')]
    reduce_scatter x1, waiting for transfers between devices: 11.3 us -> 8.73 us  [on_device(): lax.psum_scatter(partial_value, 'prefix', scatter_dimension=1, tiled=True)]
    unnamed x58 -> x62, local copies, waits for them, and re-layouts: 9.16 us -> 9.81 us
where the time goes in v1:
time: 148 us; the launch traced here: 147 us
  blocking collectives  64.4 us (44%)
  between operations  28.8 us (19%)
  local copies, waits for them, and re-layouts  18.3 us (12%)
  other arithmetic  16.3 us (11%)
  matrix products  10.8 us (7%)
  waiting for transfers between devices  8.75 us (6%)
    psum x1, blocking collectives, on_device(): grad_prompt = lax.psum(owned, 'resp').astype(jnp.bfloat16)  24.7 us
    psum x2, blocking collectives, on_device(): pair_sums = lax.psum(lax.psum(contrib, 'resp'), 'prefix')  24.1 us
    all_gather x1, blocking collectives, on_device(): full_kv = lax.all_gather(prompt_kv, 'prefix', axis=1, tiled=True)  15.6 us
    unnamed x62, local copies, waits for them, and re-layouts  9.81 us
    reduce_scatter x1, waiting for transfers between devices, on_device(): lax.psum_scatter(partial_value, 'prefix', scatter_dimension=1, tiled=True)  8.73 us
  transfers between devices with their start and end apart: 1, of which 1 were waited for; matrix products, arithmetic and copies ran while one was open for 4% of the time, Pallas kernels for 0%

profile of v1, /device:TPU:0, one launch (start us, length us, event | category | flops | bytes accessed | tf_op | source)
XLA Modules:
  0.0 147.4 jit_solution(17230850235877271238)
XLA Ops:
  7.2 1.3 fusion.48
  15.1 0.6 fusion.47
  18.3 1.9 %iota_compare_fusion.1 = (pred[2]{0:T(512)(128)(4,1)}, pred[2]{0:T(512)(128)(4,1)}) fusion(s32[]{:T(128)} %bitcast.23, s32[]{:T(128)} %bitcast.2), kind=kLoop, calls=%fused_computation.89 | loop fusion | flops 4 | bytes 12 | tf_op jit(solution)/shard_map/eq | solution.py:167
  21.5 0.6 copy-done.25
  22.2 0.6 fusion.46
  22.8 1.2 compare_convert_fusion.1
  23.9 1.2 compare_convert_fusion
  25.2 15.6 %all_gather.3 = bf16[2,128,512]{2,1,0:T(8,128)(2,1)S(1)} all-gather(bf16[2,32,512]{2,1,0:T(8,128)(2,1)S(1)} %copy-done.21), channel_id=1, replica_groups=mesh['prefix'=4,'resp'=8] {'prefix'}, dimensions={1}, use_global_device_ids=true | all-gather | bytes 327680 | tf_op jit(solution)/shard_map/all_gather | solution.py:67
  42.7 0.4 copy-done.19
  43.4 0.6 fusion.44
  45.7 1.1 divide_convert_fusion.1
  48.2 0.8 copy-done.13
  49.1 1.4 slice_convert_fusion.1
  50.5 1.5 copy.68
  52.3 1.3 multiply_reduce_fusion.3
  53.5 1.2 fusion.36
  54.7 1.5 copy.79
  56.2 1.2 convolution_bitcast_fusion.2
  57.4 1.2 multiply_reduce_fusion.2
  58.7 1.2 fusion.37
  61.1 12.0 %psum.21 = f32[32]{0:T(128)S(1)} all-reduce(f32[32]{0:T(128)S(1)} %fusion.38), channel_id=1, replica_groups=mesh['prefix'=4,'resp'=8] {'resp'}, use_global_device_ids=true, to_apply=%region_12.13 | all-reduce | flops 32 | bytes 256 | tf_op jit(solution)/shard_map/psum | solution.py:92
  73.1 12.1 %psum.22 = f32[32]{0:T(128)S(1)} all-reduce(f32[32]{0:T(128)S(1)} %psum.21), channel_id=1, replica_groups=mesh['prefix'=4,'resp'=8] {'prefix'}, use_global_device_ids=true, to_apply=%region_13.14 | all-reduce | flops 32 | bytes 256 | tf_op jit(solution)/shard_map/psum | solution.py:92
  85.2 0.5 divide_multiply_fusion
  85.7 0.6 fusion.45
  87.6 0.6 copy-done.28
  88.2 1.4 multiply_reduce_fusion.1
  89.9 0.4 fusion.25
  90.6 0.5 copy-done.8
  91.2 0.7 copy-done.27
  91.9 1.4 multiply_reduce_fusion
  93.6 0.4 fusion.23
  94.3 0.5 copy-done.10
  94.9 0.6 copy-done.22
  95.6 0.9 select_add_fusion
  96.5 1.0 copy-done.3
  97.5 0.9 fusion.29
  98.5 0.4 fusion.24
  98.8 0.6 copy-done.1
  99.8 0.5 copy-done.14
  100.3 0.4 fusion.22
  101.3 0.6 copy-done.20
  102.6 0.3 copy-done.11
  103.0 0.4 copy-done.18
  104.2 0.7 copy-done.9
  105.4 0.7 maximum_maximum_fusion
  106.1 1.0 pad_maximum_fusion
  107.1 8.7 %reduce-scatter.2.cloned.1.call-done = f32[2,32,512]{2,1,0:T(8,128)} async-done(((f32[2,128,512]{2,1,0:T(8,128)}), f32[2,32,512]{2,1,0:T(8,128)}) %reduce-scatter.2.cloned.1.call-update) | async-done | bytes 131088 | tf_op jit(solution)/shard_map/reduce_scatter | solution.py:171
  115.9 24.7 %all-reduce.1 = bf16[2,32,512]{2,1,0:T(8,128)(2,1)} all-reduce(f32[2,32,512]{2,1,0:T(8,128)} %reduce-scatter.2.cloned.1.call-done), channel_id=1, replica_groups=mesh['prefix'=4,'resp'=8] {'resp'}, use_global_device_ids=true, to_apply=%region_17.18 | all-reduce | flops 32768 | bytes 196608 | tf_op jit(solution)/shard_map/psum | solution.py:172
  (93 shorter events, 8.5 us)
Async XLA Ops:
  7.2 108.7 %reduce-scatter.2.cloned.1.call-start = ((), (), s32[]{:S(2)}) async-start(), calls=%async_computation.1 | async-start | bytes 655360 | tf_op jit(solution)/shard_map/reduce_scatter | solution.py:171
  13.1 2.1 %copy-start.24 = (s32[32]{0:T(128)S(1)}, s32[32]{0:T(128)}, u32[]{:S(2)}) copy-start(s32[32]{0:T(128)} %param.14) | copy-start | bytes 388
  13.7 11.4 %copy-start.21 = (bf16[2,32,512]{2,1,0:T(8,128)(2,1)S(1)}, bf16[2,32,512]{2,1,0:T(8,128)(2,1)}, u32[]{:S(2)}) copy-start(bf16[2,32,512]{2,1,0:T(8,128)(2,1)} %param.8) | copy-start | bytes 196612
  21.5 0.7 copy-start.25
  42.2 1.0 copy-start.19
  42.4 4.7 %copy-start.15 = (bf16[128,256]{0,1:T(8,128)(2,1)}, bf16[128,256]{0,1:T(8,128)(2,1)S(1)}, u32[]{:S(2)}) copy-start(bf16[128,256]{0,1:T(8,128)(2,1)S(1)} %copy.59) | copy-start | bytes 196612
  42.4 1.6 %copy-start.12 = (bf16[2,128,1792]{2,1,0:T(8,128)(2,1)S(1)}, bf16[2,128,1792]{2,1,0:T(8,128)(2,1)}, u32[]{:S(2)}) copy-start(bf16[2,128,1792]{2,1,0:T(8,128)(2,1)} %param.9) | copy-start | bytes 2752516
  42.6 2.1 %copy-start.17 = (bf16[128,256]{0,1:T(8,128)(2,1)}, bf16[128,256]{0,1:T(8,128)(2,1)S(1)}, u32[]{:S(2)}) copy-start(bf16[128,256]{0,1:T(8,128)(2,1)S(1)} %copy.70) | copy-start | bytes 196612
  46.8 9.4 %copy-start = (bf16[2,7,128,128]{2,3,1,0:T(8,128)(2,1)}, bf16[2,7,128,128]{2,3,1,0:T(8,128)(2,1)S(1)}, u32[]{:S(2)}) copy-start(bf16[2,7,128,128]{2,3,1,0:T(8,128)(2,1)S(1)} %get-tuple-element.33) | copy-start | bytes 1376260
  47.9 1.2 copy-start.13
  49.1 2.9 %copy-start.2 = (bf16[2,7,128,128]{2,3,1,0:T(8,128)(2,1)}, bf16[2,7,128,128]{2,3,1,0:T(8,128)(2,1)S(1)}, u32[]{:S(2)}) copy-start(bf16[2,7,128,128]{2,3,1,0:T(8,128)(2,1)S(1)} %get-tuple-element.31) | copy-start | bytes 1376260
  49.1 3.2 %copy-start.6 = (bf16[2,7,128,128]{2,3,1,0:T(8,128)(2,1)}, bf16[2,7,128,128]{2,3,1,0:T(8,128)(2,1)S(1)}, u32[]{:S(2)}) copy-start(bf16[2,7,128,128]{2,3,1,0:T(8,128)(2,1)S(1)} %get-tuple-element.30) | copy-start | bytes 1376260
  56.2 1.2 copy-start.4
  73.1 12.1 %copy-start.26 = (f32[32]{0:T(128)S(1)}, f32[32]{0:T(128)}, u32[]{:S(2)}) copy-start(f32[32]{0:T(128)} %param.15) | copy-start | bytes 388
  87.6 0.6 copy-start.28
  88.2 1.4 copy-start.7
  90.3 0.8 copy-start.8
  91.2 0.7 copy-start.27
  91.9 1.4 copy-start.5
  94.0 0.8 copy-start.10
  94.9 0.7 copy-start.22
  94.9 0.7 copy-start.23
  96.5 1.0 copy-start.3
  98.5 1.0 copy-start.1
  99.5 0.8 copy-start.14
  101.0 0.8 copy-start.20
  101.9 1.0 copy-start.11
  102.5 0.9 copy-start.18
  103.9 1.0 copy-start.9
  103.9 1.0 copy-start.16
Sparse Core Ops, SparseCore 0:
  96.7 19.1 reduce-scatter.1
